TPU v7x, 32 devices: a whole 2x2x4 slice. The times are simulated.
32 devices in a mesh: sx: 8 (over z, y), sy: 4 (over x, core).
Axes of the slice: x: 2, y: 2, z: 4, core: 2. Of those that a mesh axis runs over, the one named last changes fastest.
Arguments:
- tensors: bfloat16 [2, 8, 4, 1024, 256], P(None, 'sx', 'sy'), may hold values from -6 to 6
- gates: bfloat16 [5, 2, 2, 256, 256], replicated, may hold values from -0.1875 to 0.1875
- closing_rows: bfloat16 [2, 4096, 1024], P(None, ('sx', 'sy')), may hold values from -0.125 to 0.125
- closing_columns: float32 [2, 4096, 256], P(None, ('sx', 'sy')), may hold values from -0.25 to 0.25
Outputs:
- amplitudes: float32 [2, 4096], replicated
All inputs are finite; a program needn't handle non-finite values.
Results may differ from a plain program's by a relative error of at most 0.012.
Values may be sent and summed in bfloat16 or wider, within the bound.
A program may use at most 64 MiB of HBM per device.

v0:
```python
import jax
import jax.numpy as jnp
from jax import lax
from jax.sharding import PartitionSpec as P


def mixing_matrix(gate_pair, sign):
    own_top = jnp.concatenate([gate_pair[0, 0], gate_pair[0, 1]], axis=1)
    own_low = jnp.concatenate([-gate_pair[0, 1], gate_pair[0, 0]], axis=1)
    far_top = jnp.concatenate([gate_pair[1, 0], gate_pair[1, 1]], axis=1) * sign
    far_low = jnp.concatenate([-gate_pair[1, 1], gate_pair[1, 0]], axis=1) * sign
    return jnp.concatenate([own_top, own_low, far_top, far_low], axis=0)


def combine(own, partner, matrix):
    width = own.shape[-1]
    leading = own.shape[1:-1]
    joined = jnp.concatenate([own[0], own[1], partner[0], partner[1]], axis=-1).reshape(
        -1, 4 * width
    )
    result = jnp.dot(joined, matrix, preferred_element_type=jnp.float32).astype(jnp.bfloat16)
    real_part = result[:, :width].reshape(leading + (width,))
    imag_part = result[:, width:].reshape(leading + (width,))
    return jnp.stack([real_part, imag_part])


def local_section(grouped, gate_pair, axis_dim, bit_pos):
    shape = grouped.shape
    count = shape[axis_dim]
    split = shape[:axis_dim] + (count >> bit_pos + 1, 2, 1 << bit_pos) + shape[axis_dim + 1 :]
    blocks = grouped.reshape(split)
    lower = lax.index_in_dim(blocks, 0, axis_dim + 1, keepdims=False)
    upper = lax.index_in_dim(blocks, 1, axis_dim + 1, keepdims=False)
    new_lower = combine(lower, upper, mixing_matrix(gate_pair, 1.0))
    new_upper = combine(upper, lower, mixing_matrix(gate_pair, -1.0))
    return jnp.stack([new_lower, new_upper], axis=axis_dim + 1).reshape(shape)


def close_columns(projected, closing_columns):
    amp_real = jnp.sum(
        projected[0] * closing_columns[0] - projected[1] * closing_columns[1], axis=-1
    )
    amp_imag = jnp.sum(
        projected[0] * closing_columns[1] + projected[1] * closing_columns[0], axis=-1
    )
    return jnp.stack([amp_real, amp_imag])


def combine_rows(closing_rows, current):
    proj_real = jnp.dot(closing_rows[0], current[0], preferred_element_type=jnp.float32) - jnp.dot(
        closing_rows[1], current[1], preferred_element_type=jnp.float32
    )
    proj_imag = jnp.dot(closing_rows[0], current[1], preferred_element_type=jnp.float32) + jnp.dot(
        closing_rows[1], current[0], preferred_element_type=jnp.float32
    )
    return jnp.stack([proj_real, proj_imag])


def local(tensors, gates, closing_rows, closing_columns):
    current = tensors[:, 0, 0]
    rows_dev = current.shape[1]
    width = current.shape[2]
    count_x = lax.axis_size("sx")
    count_y = lax.axis_size("sy")
    bits_x = count_x.bit_length() - 1
    bits_y = count_y.bit_length() - 1
    grouped = lax.all_to_all(
        current.reshape(2, count_x, rows_dev // count_x, width),
        "sx",
        split_axis=1,
        concat_axis=1,
        tiled=True,
    )
    for bit_pos in range(bits_x):
        grouped = local_section(grouped, gates[bit_pos], 1, bit_pos)
    current = lax.all_to_all(grouped, "sx", split_axis=1, concat_axis=1, tiled=True).reshape(
        2, rows_dev, width
    )
    grouped = lax.all_to_all(
        current.reshape(2, count_y, rows_dev // count_y, width),
        "sy",
        split_axis=1,
        concat_axis=1,
        tiled=True,
    )
    for bit_pos in range(bits_y):
        grouped = local_section(grouped, gates[bits_x + bit_pos], 1, bit_pos)
    current = lax.all_to_all(grouped, "sy", split_axis=1, concat_axis=1, tiled=True).reshape(
        2, rows_dev, width
    )
    closed = close_columns(combine_rows(closing_rows, current), closing_columns)
    return lax.all_gather(closed, ("sx", "sy"), axis=1, tiled=True)


def solution(mesh):
    placed = (
        P(None, "sx", "sy", None, None),
        P(),
        P(None, ("sx", "sy"), None),
        P(None, ("sx", "sy"), None),
    )
    return jax.shard_map(local, mesh=mesh, in_specs=placed, out_specs=P(), check_vma=False)
```

profile of v0, /device:TPU:0, one launch (start us, length us, event | category | flops | bytes accessed | tf_op | source)
XLA Modules:
  0.0 157.4 jit_solution(10815839486201930402)
XLA Ops:
  0.0 2.3 %copy.47 = bf16[2,8,128,256]{3,2,0,1:T(8,128)(2,1)} copy(bf16[2,8,128,256]{3,2,1,0:T(8,128)(2,1)} %bitcast.207) | data formatting | bytes 2097152 | tf_op jit(solution)/shard_map/reshape;squeeze | solution.py:68
  2.3 7.3 %all-to-all-start = ((bf16[2,8,128,256]{3,2,0,1:T(8,128)(2,1)}), bf16[2,8,128,256]{3,2,0,1:T(8,128)(2,1)S(1)}, u32[]{:S(2)}, u32[]{:S(2)}) async-start(bf16[2,8,128,256]{3,2,0,1:T(8,128)(2,1)} %copy.47), calls=%async_computation | async-start | bytes 2097152 | tf_op jit(solution)/shard_map/all_to_all | solution.py:67
  9.6 1.9 %slice_bitcast_fusion = (bf16[2,2,256,256]{3,2,1,0:T(8,128)(2,1)S(1)}, bf16[2,2,256,256]{3,2,1,0:T(8,128)(2,1)S(1)}, bf16[2,2,256,256]{3,2,1,0:T(8,128)(2,1)S(1)...) fusion(bf16[5,2,2,256,256]{4,3,2,1,0:T(8,128)(2,1)} %param.5), kind=kLoop, calls=%fused_computation.162 | loop fusion | bytes 5242880 | tf_op jit(solution)/shard_map/squeeze | solution.py:87
  11.5 0.7 slice_bitcast_fusion.23
  12.2 0.7 fusion.156
  13.0 0.9 maximum_multiply_fusion
  13.9 0.8 slice_bitcast_fusion.15
  14.7 0.9 maximum_multiply_fusion.2
  15.6 0.8 fusion.160
  16.3 0.9 maximum_multiply_fusion.4
  17.2 18.2 %all-to-all-done = bf16[2,8,128,256]{3,2,0,1:T(8,128)(2,1)S(1)} async-done(((bf16[2,8,128,256]{3,2,0,1:T(8,128)(2,1)}), bf16[2,8,128,256]{3,2,0,1:T(8,128)(2,1)S(1)}, u32[]{:S(2)}, u32[]{:S(2)}) %all-to-all-start) | async-done | bytes 1048608 | tf_op jit(solution)/shard_map/all_to_all | solution.py:67
  35.5 0.8 copy-done.23
  36.4 0.7 convolution_convert_fusion.9
  37.2 0.2 copy-done.5
  37.5 0.7 convolution_convert_fusion.8
  38.6 0.7 copy-done.11
  39.4 0.7 convolution_convert_fusion.7
  40.1 0.2 copy-done.3
  40.4 0.7 convolution_convert_fusion.6
  41.4 0.1 pad_maximum_fusion
  41.6 0.7 copy-done.10
  42.3 0.7 convolution_convert_fusion.5
  43.0 0.2 copy-done.1
  43.4 0.7 convolution_convert_fusion.4
  44.3 0.1 pad_maximum_fusion.1
  44.5 29.3 %all_to_all.20 = bf16[2,8,128,256]{3,2,0,1:T(8,128)(2,1)S(1)} all-to-all(bf16[2,8,128,256]{3,2,0,1:T(8,128)(2,1)S(1)} %copy.56), channel_id=1, replica_groups=mesh['sx'=8,'sy'=4] {'sx'}, dimensions={1} | all-to-all | bytes 2097152 | tf_op jit(solution)/shard_map/all_to_all | solution.py:76
  73.9 1.1 copy.58
  75.0 3.5 %all-to-all-start.2 = ((bf16[2,4,256,256]{3,2,0,1:T(8,128)(2,1)}), bf16[2,4,256,256]{3,2,0,1:T(8,128)(2,1)S(1)}, u32[]{:S(2)}, u32[]{:S(2)}) async-start(bf16[2,4,256,256]{3,2,0,1:T(8,128)(2,1)} %copy.58), calls=%async_computation.2 | async-start | bytes 2097152 | tf_op jit(solution)/shard_map/all_to_all | solution.py:79
  78.5 0.8 slice_bitcast_fusion.7
  79.3 0.9 maximum_multiply_fusion.6
  80.1 0.7 fusion.164
  80.9 12.0 %all-to-all-done.2 = bf16[2,4,256,256]{3,2,0,1:T(8,128)(2,1)S(1)} async-done(((bf16[2,4,256,256]{3,2,0,1:T(8,128)(2,1)}), bf16[2,4,256,256]{3,2,0,1:T(8,128)(2,1)S(1)}, u32[]{:S(2)}, u32[]{:S(2)}) %all-to-all-start.2) | async-done | bytes 1048608 | tf_op jit(solution)/shard_map/all_to_all | solution.py:79
  93.0 0.7 convolution_convert_fusion.3
  93.8 0.2 copy-done.7
  94.1 0.7 convolution_convert_fusion.2
  95.3 0.7 copy-done.13
  96.0 0.7 convolution_convert_fusion.1
  96.7 0.7 convolution_convert_fusion
  97.7 0.1 pad_maximum_fusion.2
  97.8 1.1 copy.65
  98.9 3.5 %all-to-all-start.3 = ((bf16[2,4,256,256]{3,2,0,1:T(8,128)(2,1)}), bf16[2,4,256,256]{3,2,0,1:T(8,128)(2,1)S(1)}, u32[]{:S(2)}, u32[]{:S(2)}) async-start(bf16[2,4,256,256]{3,2,0,1:T(8,128)(2,1)} %copy.65), calls=%async_computation.3 | async-start | bytes 2097152 | tf_op jit(solution)/shard_map/all_to_all | solution.py:88
  102.6 14.2 %all-to-all-done.3 = bf16[2,4,256,256]{3,2,0,1:T(8,128)(2,1)S(1)} async-done(((bf16[2,4,256,256]{3,2,0,1:T(8,128)(2,1)}), bf16[2,4,256,256]{3,2,0,1:T(8,128)(2,1)S(1)}, u32[]{:S(2)}, u32[]{:S(2)}) %all-to-all-start.3) | async-done | bytes 1048608 | tf_op jit(solution)/shard_map/all_to_all | solution.py:88
  116.9 0.3 fusion.136
  117.2 0.3 fusion.134
  117.5 0.3 fusion.1
  117.9 0.4 fusion.143
  118.3 38.6 %all_gather.3 = f32[2,4096]{1,0:T(2,128)S(1)} all-gather(f32[2,128]{1,0:T(2,128)S(1)} %pad_maximum_fusion.3), channel_id=1, replica_groups=mesh['sx'=8,'sy'=4] {'sx','sy'}, dimensions={1}, use_global_device_ids=true | all-gather | bytes 33792 | tf_op jit(solution)/shard_map/all_gather | solution.py:92
  156.8 0.6 copy.78
  (81 shorter events, 2.8 us)
Async XLA Ops:
  2.3 33.1 %all-to-all-start = ((bf16[2,8,128,256]{3,2,0,1:T(8,128)(2,1)}), bf16[2,8,128,256]{3,2,0,1:T(8,128)(2,1)S(1)}, u32[]{:S(2)}, u32[]{:S(2)}) async-start(bf16[2,8,128,256]{3,2,0,1:T(8,128)(2,1)} %copy.47), calls=%async_computation | async-start | bytes 2097152 | tf_op jit(solution)/shard_map/all_to_all | solution.py:67
  35.4 0.9 copy-start.23
  35.4 1.0 copy-start.24
  35.4 1.0 copy-start.25
  36.4 0.9 copy-start.5
  36.4 1.0 copy-start.6
  38.4 0.9 copy-start.11
  38.4 1.0 copy-start.12
  38.4 1.0 copy-start.22
  39.4 0.9 copy-start.3
  39.4 1.0 copy-start.4
  41.4 0.9 copy-start.10
  41.4 1.0 copy-start.21
  42.3 0.9 copy-start.1
  42.3 1.0 copy-start.2
  75.0 17.9 %all-to-all-start.2 = ((bf16[2,4,256,256]{3,2,0,1:T(8,128)(2,1)}), bf16[2,4,256,256]{3,2,0,1:T(8,128)(2,1)S(1)}, u32[]{:S(2)}, u32[]{:S(2)}) async-start(bf16[2,4,256,256]{3,2,0,1:T(8,128)(2,1)} %copy.58), calls=%async_computation.2 | async-start | bytes 2097152 | tf_op jit(solution)/shard_map/all_to_all | solution.py:79
  79.2 13.7 %copy-start.14 = (bf16[256,256]{1,0:T(8,128)(2,1)S(1)}, bf16[256,256]{1,0:T(8,128)(2,1)}, u32[]{:S(2)}) copy-start(bf16[256,256]{1,0:T(8,128)(2,1)} %get-tuple-element.96) | copy-start | bytes 393220
  79.2 13.7 %copy-start.16 = (bf16[256,256]{1,0:T(8,128)(2,1)S(1)}, bf16[256,256]{1,0:T(8,128)(2,1)}, u32[]{:S(2)}) copy-start(bf16[256,256]{1,0:T(8,128)(2,1)} %get-tuple-element.99) | copy-start | bytes 393220
  79.2 13.7 %copy-start.19 = (bf16[256,256]{1,0:T(8,128)(2,1)S(1)}, bf16[256,256]{1,0:T(8,128)(2,1)}, u32[]{:S(2)}) copy-start(bf16[256,256]{1,0:T(8,128)(2,1)} %get-tuple-element.107) | copy-start | bytes 393220
  93.0 1.0 copy-start.7
  93.0 1.0 copy-start.8
  93.0 1.0 copy-start.15
  93.0 1.1 copy-start.17
  93.0 1.1 copy-start.20
  95.0 0.9 copy-start.13
  95.1 1.0 copy-start.18
  97.8 4.6 %copy-start.9 = (f32[2,128,256]{2,1,0:T(8,128)S(1)}, f32[2,128,256]{2,1,0:T(8,128)}, u32[]{:S(2)}) copy-start(f32[2,128,256]{2,1,0:T(8,128)} %param.7) | copy-start | bytes 786436
  98.9 17.9 %all-to-all-start.3 = ((bf16[2,4,256,256]{3,2,0,1:T(8,128)(2,1)}), bf16[2,4,256,256]{3,2,0,1:T(8,128)(2,1)S(1)}, u32[]{:S(2)}, u32[]{:S(2)}) async-start(bf16[2,4,256,256]{3,2,0,1:T(8,128)(2,1)} %copy.65), calls=%async_computation.3 | async-start | bytes 2097152 | tf_op jit(solution)/shard_map/all_to_all | solution.py:88
  102.4 14.5 %copy-start = (bf16[2,128,1024]{2,1,0:T(8,128)(2,1)S(1)}, bf16[2,128,1024]{2,1,0:T(8,128)(2,1)}, u32[]{:S(2)}) copy-start(bf16[2,128,1024]{2,1,0:T(8,128)(2,1)} %param.6) | copy-start | bytes 1572868
where the time goes:
time: 158 us; the launch traced here: 157 us
  blocking collectives  67.9 us (43%)
  waiting for transfers between devices  44.3 us (28%)
  local copies, waits for them, and re-layouts  15.1 us (10%)
  starting transfers between devices  14.3 us (9%)
  matrix products  8.46 us (5%)
  other arithmetic  6.72 us (4%)
    all_gather x1, blocking collectives, local(): return lax.all_gather(closed, ('sx', 'sy'), axis=1, tiled=True)  38.6 us
    all_to_all x1, blocking collectives, local(): lax.all_to_all(grouped, 'sx', split_axis=1, concat_axis=1, tiled=True)  29.3 us
    all_to_all x1, waiting for transfers between devices, local(): lax.all_to_all(current.reshape(2, count_x, rows_dev // count_x, width), '...  18.2 us
    all_to_all x1, waiting for transfers between devices, local(): lax.all_to_all(grouped, 'sy', split_axis=1, concat_axis=1, tiled=True)  14.2 us
    all_to_all x1, waiting for transfers between devices, local(): lax.all_to_all(current.reshape(2, count_y, rows_dev // count_y, width), '...  12 us
    all_to_all x1, starting transfers between devices, local(): lax.all_to_all(current.reshape(2, count_x, rows_dev // count_x, width), '...  7.31 us
    dot_general x10, matrix products, combine(): jnp.dot(joined, matrix, preferred_element_type=jnp.float32)  7.1 us
    unnamed x59, local copies, waits for them, and re-layouts  5.51 us
  transfers between devices with their start and end apart: 3, of which 3 were waited for; matrix products, arithmetic and copies ran while one was open for 6% of the time, Pallas kernels for 0%

commit v1 on v0

--- a/solution.py
+++ b/solution.py
@@ -64,13 +64,10 @@
     count_y = lax.axis_size("sy")
     bits_x = count_x.bit_length() - 1
     bits_y = count_y.bit_length() - 1
-    grouped = lax.all_to_all(
-        current.reshape(2, count_x, rows_dev // count_x, width),
-        "sx",
-        split_axis=1,
-        concat_axis=1,
-        tiled=True,
-    )
+    block = current.reshape(2, count_x, rows_dev // count_x, width)
+    pieces = jnp.split(block, lax.axis_size("sx"), axis=1)
+    received = lax.all_to_all(jnp.stack(pieces), "sx", 0, 0)
+    grouped = jnp.concatenate(received, axis=1)
     for bit_pos in range(bits_x):
         grouped = local_section(grouped, gates[bit_pos], 1, bit_pos)
     current = lax.all_to_all(grouped, "sx", split_axis=1, concat_axis=1, tiled=True).reshape(

time: 158 us -> 168 us (1.063)
  local copies, waits for them, and re-layouts: 15.1 us -> 24.9 us
    unnamed x59 -> x54, local copies, waits for them, and re-layouts: 5.51 us -> 16.1 us
where the time goes in v1:
time: 168 us; the launch traced here: 167 us
  blocking collectives  67.9 us (40%)
  waiting for transfers between devices  45 us (27%)
  local copies, waits for them, and re-layouts  24.9 us (15%)
  starting transfers between devices  14.3 us (9%)
  matrix products  8.45 us (5%)
  other arithmetic  6.08 us (4%)
    all_gather x1, blocking collectives, local(): return lax.all_gather(closed, ('sx', 'sy'), axis=1, tiled=True)  38.6 us
    all_to_all x1, blocking collectives, local(): lax.all_to_all(grouped, 'sx', split_axis=1, concat_axis=1, tiled=True)  29.3 us
    all_to_all x1, waiting for transfers between devices, local(): received = lax.all_to_all(jnp.stack(pieces), 'sx', 0, 0)  18.2 us
    unnamed x54, local copies, waits for them, and re-layouts  16.1 us
    all_to_all x1, waiting for transfers between devices, local(): lax.all_to_all(grouped, 'sy', split_axis=1, concat_axis=1, tiled=True)  14.2 us
    all_to_all x1, waiting for transfers between devices, local(): lax.all_to_all(current.reshape(2, count_y, rows_dev // count_y, width), '...  12.6 us
    all_to_all x1, starting transfers between devices, local(): received = lax.all_to_all(jnp.stack(pieces), 'sx', 0, 0)  7.31 us
    dot_general x10, matrix products, combine(): jnp.dot(joined, matrix, preferred_element_type=jnp.float32)  7.08 us
  transfers between devices with their start and end apart: 3, of which 3 were waited for; matrix products, arithmetic and copies ran while one was open for 6% of the time, Pallas kernels for 0%

profile of v1, /device:TPU:0, one launch (start us, length us, event | category | flops | bytes accessed | tf_op | source)
XLA Modules:
  0.0 167.2 jit_solution(9072420165900422877)
XLA Ops:
  0.0 1.6 fusion.149
  1.6 1.6 fusion.148
  3.1 1.6 fusion.147
  4.7 1.6 fusion.146
  6.3 1.6 fusion.145
  7.8 1.6 fusion.144
  9.4 1.6 fusion.143
  11.0 1.6 fusion.142
  12.5 7.3 %all-to-all-start = ((bf16[8,2,1,128,256]{4,3,1,2,0:T(8,128)(2,1)}), bf16[8,2,1,128,256]{4,3,1,2,0:T(8,128)(2,1)S(1)}, u32[]{:S(2)}, u32[]{:S(2)}) async-start(bf16[8,2,1,128,256]{4,3,1,2,0:T(8,128)(2,1)} %fusion.142), calls=%async_computation | async-start | bytes 2097152 | tf_op jit(solution)/shard_map/all_to_all | solution.py:69
  19.8 1.9 %slice_bitcast_fusion = (bf16[2,2,256,256]{3,2,1,0:T(8,128)(2,1)S(1)}, bf16[2,2,256,256]{3,2,1,0:T(8,128)(2,1)S(1)}, bf16[2,2,256,256]{3,2,1,0:T(8,128)(2,1)S(1)...) fusion(bf16[5,2,2,256,256]{4,3,2,1,0:T(8,128)(2,1)} %param.5), kind=kLoop, calls=%fused_computation.162 | loop fusion | bytes 5242880 | tf_op jit(solution)/shard_map/squeeze | solution.py:84
  21.7 0.7 slice_bitcast_fusion.23
  22.4 0.7 fusion.164
  23.2 0.9 maximum_multiply_fusion
  24.1 0.8 slice_bitcast_fusion.15
  24.9 0.9 maximum_multiply_fusion.2
  25.8 0.7 fusion.168
  26.5 0.9 maximum_multiply_fusion.4
  27.4 18.2 %all-to-all-done = bf16[8,2,1,128,256]{4,3,1,2,0:T(8,128)(2,1)S(1)} async-done(((bf16[8,2,1,128,256]{4,3,1,2,0:T(8,128)(2,1)}), bf16[8,2,1,128,256]{4,3,1,2,0:T(8,128)(2,1)S(1)}, u32[]{:S(2)}, u32[]{:S(2)}) %all-to-all-start) | async-done | bytes 1048608 | tf_op jit(solution)/shard_map/all_to_all | solution.py:69
  45.7 0.8 copy-done.17
  46.6 0.7 convolution_convert_fusion.9
  47.4 0.2 copy-done.5
  47.7 0.7 convolution_convert_fusion.8
  48.7 0.7 copy-done.11
  49.6 0.7 convolution_convert_fusion.7
  50.6 0.7 convolution_convert_fusion.6
  51.7 0.7 copy-done.10
  52.4 0.7 convolution_convert_fusion.5
  53.5 0.7 convolution_convert_fusion.4
  54.5 29.3 %all_to_all.20 = bf16[2,8,128,256]{3,2,0,1:T(8,128)(2,1)S(1)} all-to-all(bf16[2,8,128,256]{3,2,0,1:T(8,128)(2,1)S(1)} %copy.83), channel_id=1, replica_groups=mesh['sx'=8,'sy'=4] {'sx'}, dimensions={1} | all-to-all | bytes 2097152 | tf_op jit(solution)/shard_map/all_to_all | solution.py:73
  83.9 1.1 copy.85
  85.0 3.5 %all-to-all-start.2 = ((bf16[2,4,256,256]{3,2,0,1:T(8,128)(2,1)}), bf16[2,4,256,256]{3,2,0,1:T(8,128)(2,1)S(1)}, u32[]{:S(2)}, u32[]{:S(2)}) async-start(bf16[2,4,256,256]{3,2,0,1:T(8,128)(2,1)} %copy.85), calls=%async_computation.2 | async-start | bytes 2097152 | tf_op jit(solution)/shard_map/all_to_all | solution.py:76
  88.5 0.7 slice_bitcast_fusion.7
  89.3 0.9 maximum_multiply_fusion.6
  90.3 12.6 %all-to-all-done.2 = bf16[2,4,256,256]{3,2,0,1:T(8,128)(2,1)S(1)} async-done(((bf16[2,4,256,256]{3,2,0,1:T(8,128)(2,1)}), bf16[2,4,256,256]{3,2,0,1:T(8,128)(2,1)S(1)}, u32[]{:S(2)}, u32[]{:S(2)}) %all-to-all-start.2) | async-done | bytes 1048608 | tf_op jit(solution)/shard_map/all_to_all | solution.py:76
  103.0 0.7 convolution_convert_fusion.3
  104.0 0.7 convolution_convert_fusion.2
  105.1 0.7 copy-done.13
  105.8 0.7 convolution_convert_fusion.1
  106.6 0.7 convolution_convert_fusion
  107.6 1.1 copy.92
  108.6 3.5 %all-to-all-start.3 = ((bf16[2,4,256,256]{3,2,0,1:T(8,128)(2,1)}), bf16[2,4,256,256]{3,2,0,1:T(8,128)(2,1)S(1)}, u32[]{:S(2)}, u32[]{:S(2)}) async-start(bf16[2,4,256,256]{3,2,0,1:T(8,128)(2,1)} %copy.92), calls=%async_computation.3 | async-start | bytes 2097152 | tf_op jit(solution)/shard_map/all_to_all | solution.py:85
  112.4 14.2 %all-to-all-done.3 = bf16[2,4,256,256]{3,2,0,1:T(8,128)(2,1)S(1)} async-done(((bf16[2,4,256,256]{3,2,0,1:T(8,128)(2,1)}), bf16[2,4,256,256]{3,2,0,1:T(8,128)(2,1)S(1)}, u32[]{:S(2)}, u32[]{:S(2)}) %all-to-all-start.3) | async-done | bytes 1048608 | tf_op jit(solution)/shard_map/all_to_all | solution.py:85
  126.7 0.3 fusion.136
  127.0 0.3 fusion.134
  127.3 0.3 fusion.1
  127.7 0.4 fusion.151
  128.1 38.6 %all_gather.3 = f32[2,4096]{1,0:T(2,128)S(1)} all-gather(f32[2,128]{1,0:T(2,128)S(1)} %pad_maximum_fusion.3), channel_id=1, replica_groups=mesh['sx'=8,'sy'=4] {'sx','sy'}, dimensions={1}, use_global_device_ids=true | all-gather | bytes 33792 | tf_op jit(solution)/shard_map/all_gather | solution.py:89
  166.6 0.6 copy.119
  (76 shorter events, 3.5 us)
Async XLA Ops:
  12.5 33.1 %all-to-all-start = ((bf16[8,2,1,128,256]{4,3,1,2,0:T(8,128)(2,1)}), bf16[8,2,1,128,256]{4,3,1,2,0:T(8,128)(2,1)S(1)}, u32[]{:S(2)}, u32[]{:S(2)}) async-start(bf16[8,2,1,128,256]{4,3,1,2,0:T(8,128)(2,1)} %fusion.142), calls=%async_computation | async-start | bytes 2097152 | tf_op jit(solution)/shard_map/all_to_all | solution.py:69
  45.6 0.9 copy-start.17
  45.6 1.0 copy-start.18
  45.6 1.0 copy-start.19
  46.6 0.9 copy-start.5
  46.6 1.0 copy-start.6
  48.5 0.9 copy-start.11
  48.5 1.0 copy-start.12
  48.5 1.0 copy-start.16
  49.6 0.9 copy-start.3
  49.6 1.0 copy-start.4
  51.5 0.9 copy-start.10
  51.5 1.0 copy-start.15
  52.4 0.9 copy-start.1
  52.4 1.0 copy-start.2
  85.0 17.9 %all-to-all-start.2 = ((bf16[2,4,256,256]{3,2,0,1:T(8,128)(2,1)}), bf16[2,4,256,256]{3,2,0,1:T(8,128)(2,1)S(1)}, u32[]{:S(2)}, u32[]{:S(2)}) async-start(bf16[2,4,256,256]{3,2,0,1:T(8,128)(2,1)} %copy.85), calls=%async_computation.2 | async-start | bytes 2097152 | tf_op jit(solution)/shard_map/all_to_all | solution.py:76
  89.3 13.7 %copy-start.14 = (bf16[256,256]{1,0:T(8,128)(2,1)S(1)}, bf16[256,256]{1,0:T(8,128)(2,1)}, u32[]{:S(2)}) copy-start(bf16[256,256]{1,0:T(8,128)(2,1)} %get-tuple-element.107) | copy-start | bytes 393220
  103.0 1.0 copy-start.7
  103.0 1.0 copy-start.8
  104.9 0.9 copy-start.13
  107.6 4.6 %copy-start.9 = (f32[2,128,256]{2,1,0:T(8,128)S(1)}, f32[2,128,256]{2,1,0:T(8,128)}, u32[]{:S(2)}) copy-start(f32[2,128,256]{2,1,0:T(8,128)} %param.7) | copy-start | bytes 786436
  108.6 17.9 %all-to-all-start.3 = ((bf16[2,4,256,256]{3,2,0,1:T(8,128)(2,1)}), bf16[2,4,256,256]{3,2,0,1:T(8,128)(2,1)S(1)}, u32[]{:S(2)}, u32[]{:S(2)}) async-start(bf16[2,4,256,256]{3,2,0,1:T(8,128)(2,1)} %copy.92), calls=%async_computation.3 | async-start | bytes 2097152 | tf_op jit(solution)/shard_map/all_to_all | solution.py:85
  112.2 14.5 %copy-start = (bf16[2,128,1024]{2,1,0:T(8,128)(2,1)S(1)}, bf16[2,128,1024]{2,1,0:T(8,128)(2,1)}, u32[]{:S(2)}) copy-start(bf16[2,128,1024]{2,1,0:T(8,128)(2,1)} %param.6) | copy-start | bytes 1572868
